TPU v7x, 32 devices: a whole 2x2x4 slice. The times are simulated.
32 devices in a mesh: fsdp: 16 (over z, x, core), tp: 2 (over y).
Axes of the slice: x: 2, y: 2, z: 4, core: 2. Of those that a mesh axis runs over, the one named last changes fastest.
Arguments:
- saved_master: float32 [16384, 5120], P(('fsdp', 'tp')), may hold values from -6 to 6
- saved_first: float32 [16384, 5120], P(('fsdp', 'tp')), may hold values from -6 to 6
- saved_second: float32 [16384, 5120], P(('fsdp', 'tp')), may hold values from 0.05 to 20
- grad: bfloat16 [16384, 5120], P('fsdp', 'tp'), may hold values from -10000 to 10000
- row_target: int32 [16384], replicated, may hold values from 0 to 16383, as said below
- step: int32 [1], replicated, may hold values from 1 to 63
Outputs:
- new_master: float32 [16384, 5120], P('fsdp', 'tp')
- new_first: float32 [16384, 5120], P('fsdp', 'tp')
- new_second: float32 [16384, 5120], P('fsdp', 'tp')
- direction: float32 [16384, 5120], P('fsdp', 'tp')
Inputs may be any that keep to these rules, and one draw needn't show every extreme that they name: `row_target`: a permutation of 0 to 16383; the saved rows j * 1024 to (j + 1) * 1024 - 1 of every block j send exactly 64 rows into every new block of 1024 rows.
All inputs are finite; a program needn't handle non-finite values.
Results may differ from a plain program's by a relative error of at most 0.0003.
Values sent between devices are 32-bit elements; how exact they have to be, the bound alone decides.
A program may use at most 192 MiB of HBM per device.

v0:
```python
import math

import jax
import jax.numpy as jnp
from jax import lax
from jax.experimental import pallas as pl
from jax.experimental.pallas import tpu as pltpu
from jax.sharding import PartitionSpec as P

beta_one = 0.9
beta_two = 0.95
epsilon = 1e-08
learn_rate = 0.001
weight_decay = 0.1

LANES = 128
WEIGHTS = (2, 3, 4, 5, 4, 2)


def adam_kernel(scalars, master_ref, first_ref, second_ref, grad_ref, *refs):
    master_out, first_out, second_out, direction_out = refs[-4:]
    scale, first_fix, second_fix = scalars[0], scalars[1], scalars[2]
    clipped = scale * grad_ref[...].astype(jnp.float32)
    first_new = beta_one * first_ref[...] + (1.0 - beta_one) * clipped
    second_new = beta_two * second_ref[...] + (1.0 - beta_two) * clipped * clipped
    master = master_ref[...]
    first_hat = first_new / first_fix
    second_hat = second_new / second_fix
    direction = first_hat / (jnp.sqrt(second_hat) + epsilon) + weight_decay * master
    master_out[...] = master - learn_rate * direction
    first_out[...] = first_new
    second_out[...] = second_new
    direction_out[...] = direction


def adam_chunk(scalars, placed, grad, outs, begin, end):
    rows, columns = grad.shape
    unit = LANES if columns % LANES == 0 else columns
    count, first_unit = (end - begin) // unit, begin // unit

    def moved(shift):
        return pl.BlockSpec((rows, unit), lambda j: (0, j + shift))

    earlier = () if outs is None else tuple(outs)
    size = rows * (end - begin)
    return pl.pallas_call(
        adam_kernel,
        grid=(count,),
        out_shape=[jax.ShapeDtypeStruct((rows, columns), jnp.float32)] * 4,
        in_specs=[pl.BlockSpec(memory_space=pltpu.SMEM)]
        + [moved(0), moved(count), moved(2 * count), moved(first_unit)]
        + [pl.BlockSpec(memory_space=pl.ANY)] * len(earlier),
        out_specs=[moved(first_unit)] * 4,
        input_output_aliases={5 + i: i for i in range(len(earlier))},
        cost_estimate=pl.CostEstimate(
            flops=16 * size, bytes_accessed=30 * size, transcendentals=2 * size
        ),
        name="adam",
    )(scalars, placed, placed, placed, grad, *earlier)


def column_chunks(columns):
    unit = LANES if columns % LANES == 0 else 1
    units = columns // unit
    total, reached, edges = sum(WEIGHTS), 0, [0]
    for weight in WEIGHTS:
        reached += weight
        edge = units * reached // total
        if edge > edges[-1]:
            edges.append(edge)
    return [(a * unit, b * unit) for a, b in zip(edges[:-1], edges[1:])]


def per_device(all_rows_total, saved_master, saved_first, saved_second, grad, row_target, step):
    tp_count = lax.axis_size("tp")
    tp_index = lax.axis_index("tp")
    block_index = lax.axis_index("fsdp")
    block_rows, columns = grad.shape
    piece_rows = saved_master.shape[0]
    all_rows = row_target.shape[0]
    saved = (saved_master, saved_first, saved_second)

    mine = lax.dynamic_slice_in_dim(row_target, block_index * block_rows, block_rows)
    send_order = jnp.argsort(mine, stable=True)
    owner = send_order // piece_rows
    send_local = jnp.mod(tp_index - owner, tp_count) * piece_rows + send_order % piece_rows

    in_block = row_target // block_rows == block_index
    sort_keys = jnp.where(in_block, row_target, all_rows)
    source_block = jnp.argsort(sort_keys, stable=True)[:block_rows] // block_rows
    local = jnp.arange(block_rows, dtype=jnp.int32)
    before = (source_block[None, :] == source_block[:, None]) & (local[None, :] < local[:, None])
    pair_rows = block_rows // lax.axis_size("fsdp")
    place_order = source_block * pair_rows + jnp.sum(before.astype(jnp.int32), axis=1)

    def part_of(which, begin, end):
        options = [
            jnp.concatenate(
                [x[:, t * columns + begin : t * columns + end] for x in saved], axis=1
            )
            for t in range(tp_count)
        ]
        result = options[0]
        for t in range(1, tp_count):
            result = jnp.where(which == t, options[t], result)
        return result

    chunks = column_chunks(columns)
    shifts = range(1, tp_count)
    leaving = [
        [part_of(jnp.mod(tp_index + shift, tp_count), begin, end) for shift in shifts]
        for begin, end in chunks
    ]
    middles = []
    for index, (begin, end) in enumerate(chunks):
        pieces = [part_of(tp_index, begin, end)]
        for shift, outgoing in zip(shifts, leaving[index]):
            pairs = [(t, (t + shift) % tp_count) for t in range(tp_count)]
            pieces.append(lax.ppermute(outgoing, "tp", pairs))
        if index + 1 < len(chunks):
            pieces, leaving[index + 1] = lax.optimization_barrier((pieces, leaving[index + 1]))
        middles.append(pieces)

    grad_wide = grad.astype(jnp.float32)
    squares = lax.all_gather(jnp.sum(grad_wide * grad_wide), ("fsdp", "tp"))
    total = jnp.sum(squares)
    scale = jnp.minimum(1.0, math.sqrt(all_rows_total) / jnp.sqrt(total))

    count = step[0].astype(jnp.float32)
    scalars = jnp.stack(
        [
            scale,
            1.0 - jnp.power(jnp.float32(beta_one), count),
            1.0 - jnp.power(jnp.float32(beta_two), count),
        ]
    )
    arrived, updated = [], []
    for index, pieces in enumerate(middles):
        gathered = jnp.concatenate(pieces, axis=0)[send_local]
        if index == 0:
            gathered, scalars = lax.optimization_barrier((gathered, scalars))
        if index >= 2:
            placed = arrived[index - 2][place_order]
            earlier = updated[-1] if updated else None
            updated.append(adam_chunk(scalars, placed, grad, earlier, *chunks[index - 2]))
            gathered, arrived[-1], updated[-1] = lax.optimization_barrier(
                (gathered, arrived[-1], updated[-1])
            )
        elif index == 1:
            gathered, arrived[0] = lax.optimization_barrier((gathered, arrived[0]))
        arrived.append(
            lax.all_to_all(gathered, "fsdp", split_axis=0, concat_axis=0, tiled=True)
        )
    for index in range(len(updated), len(chunks)):
        placed = arrived[index][place_order]
        earlier = updated[-1] if updated else None
        updated.append(adam_chunk(scalars, placed, grad, earlier, *chunks[index]))
    return tuple(updated[-1])


def solution(mesh):
    in_specs = (
        P(("fsdp", "tp"), None),
        P(("fsdp", "tp"), None),
        P(("fsdp", "tp"), None),
        P("fsdp", "tp"),
        P(),
        P(),
    )
    out_specs = (P("fsdp", "tp"), P("fsdp", "tp"), P("fsdp", "tp"), P("fsdp", "tp"))

    def whole(saved_master, saved_first, saved_second, grad, row_target, step):
        def body(*args):
            return per_device(grad.shape[0] * grad.shape[1], *args)

        return jax.shard_map(
            body, mesh=mesh, in_specs=in_specs, out_specs=out_specs, check_vma=False
        )(saved_master, saved_first, saved_second, grad, row_target, step)

    return whole
```

profile of v0, /device:TPU:1, one launch (start us, length us, event | category | flops | bytes accessed | tf_op | source)
XLA Modules:
  0.0 819.1 jit_solution(8863789874913475360)
XLA Ops:
  0.7 2.8 fusion.28
  3.5 3.8 fusion.26
  10.7 3.3 multiply_reduce_fusion
  14.7 64.5 %all-reduce = f32[32]{0:T(128)S(1)} all-reduce(f32[32]{0:T(128)S(1)} %dynamic-update-slice), channel_id=1, replica_groups=mesh['fsdp'=16,'tp'=2] {'fsdp','tp'}, use_global_device_ids=true, to_apply=%add | all-reduce | flops 32 | bytes 256
  81.3 4.4 sort.34
  95.1 5.2 gather_fusion
  100.4 6.0 all-to-all-start
  107.4 4.0 fusion.31
  111.4 6.2 fusion.29
  117.5 3.0 fusion.3
  120.5 38.7 %collective-permute-done.1 = f32[512,1152]{1,0:T(8,128)S(1)} collective-permute-done((f32[512,1152]{1,0:T(8,128)}, f32[512,1152]{1,0:T(8,128)S(1)}, u32[]{:S(2)}, u32[]{:S(2)}) %collective-permute-start.1) | collective-permute-done | bytes 2359328 | tf_op jit(solution)/shard_map/ppermute | solution.py:119
  161.7 9.0 %gather_fusion.5 = f32[1024,1152]{1,0:T(8,128)} fusion(f32[1024,1152]{1,0:T(8,128)} %pad_maximum_fusion.3, s32[1024]{0:T(1024)S(1)} %fusion.22), kind=kCustom, calls=%fused_computation.5 | custom fusion | bytes 9441280 | tf_op jit(solution)/shard_map/gather | solution.py:139
  170.8 10.3 %all-to-all-start.1 = ((f32[16,64,1152]{2,1,0:T(8,128)}), f32[16,64,1152]{2,1,0:T(8,128)}, u32[]{:S(2)}, u32[]{:S(2)}) async-start(f32[16,64,1152]{2,1,0:T(8,128)} %bitcast.21), calls=%async_computation.1 | async-start | bytes 9437184 | tf_op jit(solution)/shard_map/all_to_all | solution.py:152
  182.2 7.8 sort.35
  192.4 2.9 fusion.32
  195.3 3.6 fusion.1
  198.9 52.1 %collective-permute-done.2 = f32[512,1536]{1,0:T(8,128)} collective-permute-done((f32[512,1536]{1,0:T(8,128)}, f32[512,1536]{1,0:T(8,128)}, u32[]{:S(2)}, u32[]{:S(2)}) %collective-permute-start.2) | collective-permute-done | bytes 3145760 | tf_op jit(solution)/shard_map/ppermute | solution.py:119
  250.9 5.0 pad_maximum_fusion.2
  256.0 10.6 %gather_fusion.4 = f32[1024,1536]{1,0:T(8,128)} fusion(f32[1024,1536]{1,0:T(8,128)} %pad_maximum_fusion.2, s32[1024]{0:T(1024)S(1)} %fusion.22), kind=kCustom, calls=%fused_computation.4 | custom fusion | bytes 12587008 | tf_op jit(solution)/shard_map/gather | solution.py:139
  266.5 5.3 gather_fusion.6
  271.9 3.9 adam.6
  275.8 13.7 %all-to-all-start.2 = ((f32[16,64,1536]{2,1,0:T(8,128)}), f32[16,64,1536]{2,1,0:T(8,128)}, u32[]{:S(2)}, u32[]{:S(2)}) async-start(f32[16,64,1536]{2,1,0:T(8,128)} %bitcast.19), calls=%async_computation.2 | async-start | bytes 12582912 | tf_op jit(solution)/shard_map/all_to_all | solution.py:152
  290.6 4.4 fusion.5
  295.0 81.1 %collective-permute-done.3 = f32[512,1920]{1,0:T(8,128)S(1)} collective-permute-done((f32[512,1920]{1,0:T(8,128)}, f32[512,1920]{1,0:T(8,128)S(1)}, u32[]{:S(2)}, u32[]{:S(2)}) %collective-permute-start.3) | collective-permute-done | bytes 3932192 | tf_op jit(solution)/shard_map/ppermute | solution.py:119
  376.2 3.6 pad_maximum_fusion
  379.8 12.0 %gather_fusion.3 = f32[1024,1920]{1,0:T(8,128)} fusion(f32[1024,1920]{1,0:T(8,128)} %pad_maximum_fusion, s32[1024]{0:T(1024)S(1)} %fusion.22), kind=kCustom, calls=%fused_computation.3 | custom fusion | bytes 15732736 | tf_op jit(solution)/shard_map/gather | solution.py:139
  391.7 9.0 %gather_fusion.7 = f32[1024,1152]{1,0:T(8,128)} fusion(f32[1024,1152]{1,0:T(8,128)} %bitcast.5, s32[1024]{0:T(1024)S(1)} %fusion.23), kind=kCustom, calls=%fused_computation.7 | custom fusion | bytes 9441280 | tf_op jit(solution)/shard_map/gather | solution.py:143
  400.7 6.6 adam.7
  407.4 24.3 %all-to-all-start.3 = ((f32[16,64,1920]{2,1,0:T(8,128)}), f32[16,64,1920]{2,1,0:T(8,128)}, u32[]{:S(2)}, u32[]{:S(2)}) async-start(f32[16,64,1920]{2,1,0:T(8,128)} %bitcast.18), calls=%async_computation.3 | async-start | bytes 15728640 | tf_op jit(solution)/shard_map/all_to_all | solution.py:152
  432.7 3.8 fusion.10
  436.6 64.9 %collective-permute-done.4 = f32[512,1536]{1,0:T(8,128)S(1)} collective-permute-done((f32[512,1536]{1,0:T(8,128)}, f32[512,1536]{1,0:T(8,128)S(1)}, u32[]{:S(2)}, u32[]{:S(2)}) %collective-permute-start.4) | collective-permute-done | bytes 3145760 | tf_op jit(solution)/shard_map/ppermute | solution.py:119
  501.5 3.1 pad_maximum_fusion.1
  504.6 10.6 %gather_fusion.2 = f32[1024,1536]{1,0:T(8,128)} fusion(f32[1024,1536]{1,0:T(8,128)} %pad_maximum_fusion.1, s32[1024]{0:T(1024)S(1)} %fusion.22), kind=kCustom, calls=%fused_computation.2 | custom fusion | bytes 12587008 | tf_op jit(solution)/shard_map/gather | solution.py:139
  515.2 10.5 %gather_fusion.8 = f32[1024,1536]{1,0:T(8,128)} fusion(f32[1024,1536]{1,0:T(8,128)} %bitcast.7, s32[1024]{0:T(1024)S(1)} %fusion.23), kind=kCustom, calls=%fused_computation.8 | custom fusion | bytes 12587008 | tf_op jit(solution)/shard_map/gather | solution.py:143
  525.7 7.3 adam.8
  533.0 40.8 %all-to-all-done.3 = f32[16,64,1920]{2,1,0:T(8,128)} async-done(((f32[16,64,1920]{2,1,0:T(8,128)}), f32[16,64,1920]{2,1,0:T(8,128)}, u32[]{:S(2)}, u32[]{:S(2)}) %all-to-all-start.3) | async-done | bytes 7864352 | tf_op jit(solution)/shard_map/all_to_all | solution.py:152
  573.8 34.0 %all-to-all-start.4 = ((f32[16,64,1536]{2,1,0:T(8,128)}), f32[16,64,1536]{2,1,0:T(8,128)}, u32[]{:S(2)}, u32[]{:S(2)}) async-start(f32[16,64,1536]{2,1,0:T(8,128)} %bitcast.20), calls=%async_computation.4 | async-start | bytes 12582912 | tf_op jit(solution)/shard_map/all_to_all | solution.py:152
  608.8 34.9 %collective-permute-done.5 = f32[512,768]{1,0:T(8,128)S(1)} collective-permute-done((f32[512,768]{1,0:T(8,128)S(1)}, f32[512,768]{1,0:T(8,128)S(1)}, u32[]{:S(2)}, u32[]{:S(2)}) %collective-permute-start.5) | collective-permute-done | bytes 1572896 | tf_op jit(solution)/shard_map/ppermute | solution.py:119
  645.3 5.3 gather_fusion.1
  650.7 11.9 %gather_fusion.9 = f32[1024,1920]{1,0:T(8,128)} fusion(f32[1024,1920]{1,0:T(8,128)} %bitcast.9, s32[1024]{0:T(1024)S(1)} %fusion.23), kind=kCustom, calls=%fused_computation.9 | custom fusion | bytes 15732736 | tf_op jit(solution)/shard_map/gather | solution.py:143
  662.6 10.1 %adam.9 = (f32[1024,2560]{1,0:T(8,128)}, f32[1024,2560]{1,0:T(8,128)}, f32[1024,2560]{1,0:T(8,128)}, f32[1024,2560]{1,0:T(8,128)}) custom-call(f32[3]{0:T(128)} %pad_maximum_fusion.18.scalars, f32[1024,1920]{1,0:T(8,128)} %gather_fusion.9, f32[1024,1920]{1,0:T(8,128)} %gather_fusion.9, ...), custom_call_target="tpu_custom_call", output_to_operand_aliasing={{0}: (5, {}), {1}: (6, {}), {2}: (7, {}), {3}: (8, {})} | custom-call | flops 10485760 | bytes 19660800 | tf_op jit(solution)/shard_map/adam/pallas_call | solution.py:46
  672.7 49.8 %all-to-all-done.4 = f32[16,64,1536]{2,1,0:T(8,128)} async-done(((f32[16,64,1536]{2,1,0:T(8,128)}), f32[16,64,1536]{2,1,0:T(8,128)}, u32[]{:S(2)}, u32[]{:S(2)}) %all-to-all-start.4) | async-done | bytes 6291488 | tf_op jit(solution)/shard_map/all_to_all | solution.py:152
  722.4 27.5 %all-to-all-start.5 = ((f32[16,64,768]{2,1,0:T(8,128)}), f32[16,64,768]{2,1,0:T(8,128)S(1)}, u32[]{:S(2)}, u32[]{:S(2)}) async-start(f32[16,64,768]{2,1,0:T(8,128)} %bitcast.23), calls=%async_computation.5 | async-start | bytes 6291456 | tf_op jit(solution)/shard_map/all_to_all | solution.py:152
  749.9 10.5 %gather_fusion.11 = f32[1024,1536]{1,0:T(8,128)} fusion(f32[1024,1536]{1,0:T(8,128)} %bitcast.11, s32[1024]{0:T(1024)S(1)} %fusion.23), kind=kCustom, calls=%fused_computation.11 | custom fusion | bytes 12587008 | tf_op jit(solution)/shard_map/gather | solution.py:155
  760.4 7.3 adam.10
  767.8 42.0 %all-to-all-done.5 = f32[16,64,768]{2,1,0:T(8,128)S(1)} async-done(((f32[16,64,768]{2,1,0:T(8,128)}), f32[16,64,768]{2,1,0:T(8,128)S(1)}, u32[]{:S(2)}, u32[]{:S(2)}) %all-to-all-start.5) | async-done | bytes 3145760 | tf_op jit(solution)/shard_map/all_to_all | solution.py:152
  809.7 5.3 gather_fusion.10
  815.0 3.9 adam.11
  (49 shorter events, 26.0 us)
Async XLA Ops:
  0.6 10.0 %slice-start = ((s8[5242880]{0:T(1024)(128)(4,1)}), s8[4194304]{0:T(1024)(128)(4,1)S(1)}, s32[]{:S(2)}) async-start(s8[5242880]{0:T(1024)(128)(4,1)} %bitcast.14), calls=%async_computation.6 | async-start | bytes 8388608
  3.5 7.2 slice-start.1
  8.6 72.6 %copy-start.6 = (s32[16384]{0:T(1024)S(1)}, s32[16384]{0:T(1024)}, u32[]{:S(2)}) copy-start(s32[16384]{0:T(1024)} %param.10) | copy-start | bytes 196612
  8.6 83.8 %collective-permute-start = (f32[512,768]{1,0:T(8,128)S(1)}, f32[512,768]{1,0:T(8,128)S(1)}, u32[]{:S(2)}, u32[]{:S(2)}) collective-permute-start(f32[512,768]{1,0:T(8,128)S(1)} %get-tuple-element.180), channel_id=1, source_target_pairs={{0,1},{1,0},{2,3},{3,2},{4,5},{5,4},{6,7},{7,6},{8,9},{9,8},{10,11... | collective-permute-start | bytes 4718600 | tf_op jit(solution)/shard_map/ppermute | solution.py:119
  89.8 3.7 copy-start.3
  92.4 1.1 copy-start.4
  100.4 70.4 %all-to-all-start = ((f32[16,64,768]{2,1,0:T(8,128)}), f32[16,64,768]{2,1,0:T(8,128)S(1)}, u32[]{:S(2)}, u32[]{:S(2)}) async-start(f32[16,64,768]{2,1,0:T(8,128)} %bitcast.22), calls=%async_computation | async-start | bytes 6291456 | tf_op jit(solution)/shard_map/all_to_all | solution.py:152
  106.4 52.9 %collective-permute-start.1 = (f32[512,1152]{1,0:T(8,128)}, f32[512,1152]{1,0:T(8,128)S(1)}, u32[]{:S(2)}, u32[]{:S(2)}) collective-permute-start(f32[512,1152]{1,0:T(8,128)} %get-tuple-element.73), channel_id=1, source_target_pairs={{0,1},{1,0},{2,3},{3,2},{4,5},{5,4},{6,7},{7,6},{8,9},{9,8},{10,11... | collective-permute-start | bytes 7077896 | tf_op jit(solution)/shard_map/ppermute | solution.py:119
  117.5 41.7 %copy-start.2 = (f32[512,1152]{1,0:T(8,128)S(1)}, f32[512,1152]{1,0:T(8,128)}, u32[]{:S(2)}) copy-start(f32[512,1152]{1,0:T(8,128)} %get-tuple-element.84) | copy-start | bytes 7077892
  170.8 105.0 %all-to-all-start.1 = ((f32[16,64,1152]{2,1,0:T(8,128)}), f32[16,64,1152]{2,1,0:T(8,128)}, u32[]{:S(2)}, u32[]{:S(2)}) async-start(f32[16,64,1152]{2,1,0:T(8,128)} %bitcast.21), calls=%async_computation.1 | async-start | bytes 9437184 | tf_op jit(solution)/shard_map/all_to_all | solution.py:152
  181.1 69.9 %collective-permute-start.2 = (f32[512,1536]{1,0:T(8,128)}, f32[512,1536]{1,0:T(8,128)}, u32[]{:S(2)}, u32[]{:S(2)}) collective-permute-start(f32[512,1536]{1,0:T(8,128)} %get-tuple-element.74), channel_id=1, source_target_pairs={{0,1},{1,0},{2,3},{3,2},{4,5},{5,4},{6,7},{7,6},{8,9},{9,8},{10,11... | collective-permute-start | bytes 9437192 | tf_op jit(solution)/shard_map/ppermute | solution.py:119
  195.2 55.7 %copy-start.1 = (f32[512,1536]{1,0:T(8,128)S(1)}, f32[512,1536]{1,0:T(8,128)}, u32[]{:S(2)}) copy-start(f32[512,1536]{1,0:T(8,128)} %get-tuple-element.82) | copy-start | bytes 9437188
  275.8 131.6 %all-to-all-start.2 = ((f32[16,64,1536]{2,1,0:T(8,128)}), f32[16,64,1536]{2,1,0:T(8,128)}, u32[]{:S(2)}, u32[]{:S(2)}) async-start(f32[16,64,1536]{2,1,0:T(8,128)} %bitcast.19), calls=%async_computation.2 | async-start | bytes 12582912 | tf_op jit(solution)/shard_map/all_to_all | solution.py:152
  289.5 86.6 %collective-permute-start.3 = (f32[512,1920]{1,0:T(8,128)}, f32[512,1920]{1,0:T(8,128)S(1)}, u32[]{:S(2)}, u32[]{:S(2)}) collective-permute-start(f32[512,1920]{1,0:T(8,128)} %get-tuple-element.75), channel_id=1, source_target_pairs={{0,1},{1,0},{2,3},{3,2},{4,5},{5,4},{6,7},{7,6},{8,9},{9,8},{10,11... | collective-permute-start | bytes 11796488 | tf_op jit(solution)/shard_map/ppermute | solution.py:119
  290.6 85.6 %copy-start = (f32[512,1920]{1,0:T(8,128)S(1)}, f32[512,1920]{1,0:T(8,128)}, u32[]{:S(2)}) copy-start(f32[512,1920]{1,0:T(8,128)} %get-tuple-element.80) | copy-start | bytes 11796484
  407.4 166.4 %all-to-all-start.3 = ((f32[16,64,1920]{2,1,0:T(8,128)}), f32[16,64,1920]{2,1,0:T(8,128)}, u32[]{:S(2)}, u32[]{:S(2)}) async-start(f32[16,64,1920]{2,1,0:T(8,128)} %bitcast.18), calls=%async_computation.3 | async-start | bytes 15728640 | tf_op jit(solution)/shard_map/all_to_all | solution.py:152
  431.7 69.8 %collective-permute-start.4 = (f32[512,1536]{1,0:T(8,128)}, f32[512,1536]{1,0:T(8,128)S(1)}, u32[]{:S(2)}, u32[]{:S(2)}) collective-permute-start(f32[512,1536]{1,0:T(8,128)} %get-tuple-element.76), channel_id=1, source_target_pairs={{0,1},{1,0},{2,3},{3,2},{4,5},{5,4},{6,7},{7,6},{8,9},{9,8},{10,11... | collective-permute-start | bytes 9437192 | tf_op jit(solution)/shard_map/ppermute | solution.py:119
  573.8 34.0 %copy-start.5 = (f32[512,768]{1,0:T(8,128)S(1)}, f32[512,768]{1,0:T(8,128)}, u32[]{:S(2)}) copy-start(f32[512,768]{1,0:T(8,128)} %get-tuple-element.77) | copy-start | bytes 4718596
  573.8 148.6 %all-to-all-start.4 = ((f32[16,64,1536]{2,1,0:T(8,128)}), f32[16,64,1536]{2,1,0:T(8,128)}, u32[]{:S(2)}, u32[]{:S(2)}) async-start(f32[16,64,1536]{2,1,0:T(8,128)} %bitcast.20), calls=%async_computation.4 | async-start | bytes 12582912 | tf_op jit(solution)/shard_map/all_to_all | solution.py:152
  607.8 36.0 %collective-permute-start.5 = (f32[512,768]{1,0:T(8,128)S(1)}, f32[512,768]{1,0:T(8,128)S(1)}, u32[]{:S(2)}, u32[]{:S(2)}) collective-permute-start(f32[512,768]{1,0:T(8,128)S(1)} %copy-done.5), channel_id=1, source_target_pairs={{0,1},{1,0},{2,3},{3,2},{4,5},{5,4},{6,7},{7,6},{8,9},{9,8},{10,11... | collective-permute-start | bytes 4718600 | tf_op jit(solution)/shard_map/ppermute | solution.py:119
  722.4 87.3 %all-to-all-start.5 = ((f32[16,64,768]{2,1,0:T(8,128)}), f32[16,64,768]{2,1,0:T(8,128)S(1)}, u32[]{:S(2)}, u32[]{:S(2)}) async-start(f32[16,64,768]{2,1,0:T(8,128)} %bitcast.23), calls=%async_computation.5 | async-start | bytes 6291456 | tf_op jit(solution)/shard_map/all_to_all | solution.py:152
where the time goes:
time: 830 us; the launch traced here: 819 us
  waiting for transfers between devices  404 us (49%)
  local copies, waits for them, and re-layouts  132 us (16%)
  starting transfers between devices  123 us (15%)
  blocking collectives  64.5 us (8%)
  other arithmetic  53.4 us (6%)
  Pallas kernels  39.2 us (5%)
    ppermute x6, waiting for transfers between devices, per_device(): pieces.append(lax.ppermute(outgoing, 'tp', pairs))  272 us
    all_to_all x6, waiting for transfers between devices, per_device(): lax.all_to_all(gathered, 'fsdp', split_axis=0, concat_axis=0, tiled=True)  132 us
    all_to_all x6, starting transfers between devices, per_device(): lax.all_to_all(gathered, 'fsdp', split_axis=0, concat_axis=0, tiled=True)  116 us
    unnamed x1, blocking collectives  64.5 us
    gather x6, local copies, waits for them, and re-layouts, per_device(): gathered = jnp.concatenate(pieces, axis=0)[send_local]  52.7 us
    pallas_call x6, Pallas kernels, adam_chunk(): pl.pallas_call(adam_kernel, grid=(count,), out_shape=[jax.ShapeDtypeStruc...  39.2 us
    gather x4, local copies, waits for them, and re-layouts, per_device(): placed = arrived[index - 2][place_order]  36.8 us
    slice x8, local copies, waits for them, and re-layouts, part_of(): x[:, t * columns + begin:t * columns + end]  25.1 us
  transfers between devices with their start and end apart: 12, of which 8 were waited for; matrix products, arithmetic and copies ran while one was open for 20% of the time, Pallas kernels for 4%

commit v1 on v0

v1 whole, which is shorter than its diff:
```python
import math

import jax
import jax.numpy as jnp
from jax import lax
from jax.experimental import pallas as pl
from jax.experimental.pallas import tpu as pltpu
from jax.sharding import PartitionSpec as P

beta_one = 0.9
beta_two = 0.95
epsilon = 1e-08
learn_rate = 0.001
weight_decay = 0.1

LANES = 128
STAGES = 2
SENDS = 3
ARRIVALS = 4
SLOT = 1 << 12
MESH = pl.DeviceIdType.MESH


def partner_steps(count):
    bits = count.bit_length() - 1
    if 1 << bits != count:
        return list(range(1, count))
    return [int(format(i, f"0{bits}b")[::-1], 2) for i in range(1, count)]


def restore_kernel(
    count,
    entries,
    send_idx,
    place_idx,
    fixes,
    master_ref,
    first_ref,
    second_ref,
    grad_ref,
    out,
    landed,
    stage,
    send,
    recv_0,
    recv_1,
    recv_2,
    recv_3,
    grad,
    partial,
    partial_row,
    from_tp,
    from_fsdp,
    scale_ref,
    tp_sent,
    tp_landed,
    staged,
    sent,
    arrived,
    grad_sem,
    partial_sems,
):
    tp_count, fsdp_count = count
    f, t = lax.axis_index("fsdp"), lax.axis_index("tp")
    saved = (master_ref, first_ref, second_ref)
    arrivals = (recv_0, recv_1, recv_2, recv_3)
    steps, block_rows = out.shape[1], out.shape[2]
    columns = steps * LANES
    piece = master_ref.shape[0]
    pair = block_rows // fsdp_count
    power = fsdp_count & (fsdp_count - 1) == 0

    def along_tp(d):
        return lax.rem(t + d, tp_count)

    def along_fsdp(d):
        return jnp.bitwise_xor(f, d) if power else lax.rem(f + d, fsdp_count)

    def unit(ref, half, s):
        return ref.at[:, pl.ds(pl.multiple_of(half * columns + s * LANES, LANES), LANES)]

    def tp_start(s):
        for d in range(1, tp_count):
            peer = along_tp(d)
            for x, ref in enumerate(saved):
                pltpu.make_async_remote_copy(
                    src_ref=unit(ref, peer, s),
                    dst_ref=landed.at[s, t, x],
                    send_sem=tp_sent.at[s],
                    recv_sem=tp_landed.at[s],
                    device_id=(f, peer),
                    device_id_type=MESH,
                ).start()

    def tp_wait(s, sem):
        if tp_count > 1:
            whole = landed.at[s, pl.ds(0, tp_count - 1)]
            pltpu.make_async_copy(whole, whole, sem.at[s]).wait()

    def stage_start(s):
        slot = lax.rem(s, STAGES)
        for d in range(tp_count):
            half = along_tp(d)
            for x, ref in enumerate(saved):
                rows = pl.ds(pl.multiple_of((half * 3 + x) * piece, 8), piece)
                source = unit(ref, t, s) if d == 0 else landed.at[s, half, x]
                pltpu.make_async_copy(source, stage.at[slot, rows], staged.at[slot]).start()

    def stage_wait(s):
        slot = lax.rem(s, STAGES)
        pltpu.make_async_copy(stage.at[slot], stage.at[slot], staged.at[slot]).wait()

    def with_arrival(s, body):
        for i, recv in enumerate(arrivals):
            pl.when(lax.rem(s, len(arrivals)) == i)(lambda recv=recv: body(s, recv))

    def send_start(s, recv):
        slot = lax.rem(s, SENDS)
        recv[f] = send[slot, f]
        for d in partner_steps(fsdp_count):
            peer = along_fsdp(d)
            pltpu.make_async_remote_copy(
                src_ref=send.at[slot, peer],
                dst_ref=recv.at[f],
                send_sem=sent.at[slot],
                recv_sem=arrived.at[s],
                device_id=(peer, t),
                device_id_type=MESH,
            ).start()

    def send_wait(s):
        slot = lax.rem(s, SENDS)
        whole = send.at[slot, pl.ds(0, fsdp_count - 1)]
        pltpu.make_async_copy(whole, whole, sent.at[slot]).wait()

    def recv_wait(s):
        whole = send.at[0, pl.ds(0, fsdp_count - 1)]
        pltpu.make_async_copy(whole, whole, arrived.at[s]).wait()

    run = math.gcd(pair, 8)

    def gather(s):
        source, slot = lax.rem(s, STAGES), lax.rem(s, SENDS)

        def one_block(b, carry):
            def one_run(k, carry):
                for u in range(run):
                    row = send_idx[b * pair + k * run + u]
                    for x in range(3):
                        send[slot, b, pl.ds(x * pair + k * run + u, 1), :] = stage[
                            source, pl.ds(row + x * piece, 1), :
                        ]
                return carry

            return lax.fori_loop(0, pair // run, one_run, carry)

        lax.fori_loop(0, fsdp_count, one_block, 0)

    def place(s, recv):

        def one_run(k, carry):
            for u in range(8):
                packed = place_idx[k * 8 + u]
                block, row = packed // SLOT, packed % SLOT
                for x in range(3):
                    out[x, s, pl.ds(k * 8 + u, 1), :] = recv[block, pl.ds(row + x * pair, 1), :]
            return carry

        lax.fori_loop(0, block_rows // 8, one_run, 0)

    tile = math.gcd(block_rows, 64)

    def adam(s):
        scale = scale_ref[...]
        first_fix, second_fix = fixes[0], fixes[1]

        def one_tile(k, carry):
            rows = pl.ds(pl.multiple_of(k * tile, tile), tile)
            clipped = scale * grad[s, rows, :].astype(jnp.float32)
            master = out[0, s, rows, :]
            first_new = beta_one * out[1, s, rows, :] + (1.0 - beta_one) * clipped
            second_new = beta_two * out[2, s, rows, :] + (1.0 - beta_two) * clipped * clipped
            first_hat = first_new / first_fix
            second_hat = second_new / second_fix
            direction = first_hat / (jnp.sqrt(second_hat) + epsilon) + weight_decay * master
            out[0, s, rows, :] = master - learn_rate * direction
            out[1, s, rows, :] = first_new
            out[2, s, rows, :] = second_new
            out[3, s, rows, :] = direction
            return carry

        lax.fori_loop(0, block_rows // tile, one_tile, 0)

    def square_sum():
        def one_unit(s, total):
            def one_tile(k, total):
                rows = pl.ds(pl.multiple_of(k * tile, tile), tile)
                wide = grad[s, rows, :].astype(jnp.float32)
                return total + wide * wide

            return lax.fori_loop(0, block_rows // tile, one_tile, total)

        total = lax.fori_loop(0, steps, one_unit, jnp.zeros((tile, LANES), jnp.float32))
        return jnp.sum(total, axis=0, keepdims=True)

    def partial_copies(which):
        if which == 0:
            peers = [(f, along_tp(d)) for d in range(1, tp_count)]
            source, target = partial, from_tp.at[t]
        else:
            peers = [(along_fsdp(d), t) for d in partner_steps(fsdp_count)]
            source, target = partial_row, from_fsdp.at[f]
        return [
            pltpu.make_async_remote_copy(
                src_ref=source,
                dst_ref=target,
                send_sem=partial_sems.at[2 * which],
                recv_sem=partial_sems.at[2 * which + 1],
                device_id=peer,
                device_id_type=MESH,
            )
            for peer in peers
        ]

    def partial_wait(which, side):
        held = (from_tp, from_fsdp)[which]
        members = (tp_count, fsdp_count)[which]
        if members > 1:
            whole = held.at[pl.ds(0, members - 1)]
            pltpu.make_async_copy(whole, whole, partial_sems.at[2 * which + side]).wait()

    def summed(held, members):
        total = held[0]
        for i in range(1, members):
            total = total + held[i]
        return total

    def grad_copy(s):
        return pltpu.make_async_copy(unit(grad_ref, 0, s), grad.at[s], grad_sem)

    tp_start(0)
    lax.fori_loop(0, steps, lambda s, carry: (grad_copy(s).start(), carry)[1], 0)
    pltpu.make_async_copy(grad, grad, grad_sem).wait()
    own = square_sum()
    partial[...] = own
    from_tp[t] = own
    for copy in partial_copies(0):
        copy.start()
    if steps > 1:
        tp_start(1)
    tp_wait(0, tp_landed)
    stage_start(0)

    def step(s, carry):
        @pl.when(s < steps)
        def _():
            stage_wait(s)

            @pl.when(s >= SENDS)
            def _():
                send_wait(s - SENDS)

            gather(s)
            with_arrival(s, send_start)

            @pl.when(s == 0)
            def _():
                partial_wait(0, 1)
                row = summed(from_tp, tp_count)
                partial_row[...] = row
                from_fsdp[f] = row
                for copy in partial_copies(1):
                    copy.start()

            @pl.when(s + 2 < steps)
            def _():
                tp_start(s + 2)

            @pl.when(s + 1 < steps)
            def _():
                tp_wait(s + 1, tp_landed)
                stage_start(s + 1)

        @pl.when(s >= 1)
        def _():
            recv_wait(s - 1)
            with_arrival(s - 1, place)

            @pl.when(s == 1)
            def _():
                partial_wait(1, 1)
                total = jnp.sum(summed(from_fsdp, fsdp_count), axis=1, keepdims=True)
                scale = jnp.minimum(1.0, math.sqrt(entries) / jnp.sqrt(total))
                scale_ref[...] = jnp.broadcast_to(scale, scale_ref.shape)

            adam(s - 1)

        return carry

    lax.fori_loop(0, steps + 1, step, 0)
    for s in range(max(0, steps - SENDS), steps):
        send_wait(s)
    lax.fori_loop(0, steps, lambda s, carry: (tp_wait(s, tp_sent), carry)[1], 0)
    partial_wait(0, 0)
    partial_wait(1, 0)


def drain_kernel(held, *refs):
    outs, sem = refs[:-1], refs[-1]
    copies = [
        pltpu.make_async_copy(
            held.at[i, u], out.at[:, u * LANES : (u + 1) * LANES], sem.at[i, u]
        )
        for i, out in enumerate(outs)
        for u in range(held.shape[1])
    ]
    for copy in copies:
        copy.start()
    for copy in copies:
        copy.wait()


def per_device(entries, saved_master, saved_first, saved_second, grad, row_target, step):
    tp_count, fsdp_count = lax.axis_size("tp"), lax.axis_size("fsdp")
    block_index = lax.axis_index("fsdp")
    block_rows, columns = grad.shape
    piece = saved_master.shape[0]
    all_rows = row_target.shape[0]
    pair = block_rows // fsdp_count
    steps = columns // LANES

    mine = lax.dynamic_slice_in_dim(row_target, block_index * block_rows, block_rows)
    send_order = jnp.argsort(mine, stable=True).astype(jnp.int32)
    send_idx = (send_order // piece) * (3 * piece) + send_order % piece

    in_block = row_target // block_rows == block_index
    sort_keys = jnp.where(in_block, row_target, all_rows)
    source_block = jnp.argsort(sort_keys, stable=True)[:block_rows].astype(jnp.int32) // block_rows
    local = jnp.arange(block_rows, dtype=jnp.int32)
    before = (source_block[None, :] == source_block[:, None]) & (local[None, :] < local[:, None])
    place_idx = source_block * SLOT + jnp.sum(before.astype(jnp.int32), axis=1)

    taken = step[0].astype(jnp.float32)
    fixes = jnp.stack(
        [
            1.0 - jnp.power(jnp.float32(beta_one), taken),
            1.0 - jnp.power(jnp.float32(beta_two), taken),
        ]
    )

    def kernel(*refs):
        restore_kernel((tp_count, fsdp_count), entries, *refs)

    smem = pl.BlockSpec(memory_space=pltpu.SMEM)
    hbm = pl.BlockSpec(memory_space=pltpu.HBM)
    vmem = pl.BlockSpec(memory_space=pltpu.VMEM)
    dma = pltpu.SemaphoreType.DMA
    wide = jnp.float32
    held, _ = pl.pallas_call(
        kernel,
        out_shape=[
            pltpu.VMEM((4, steps, block_rows, LANES), wide),
            jax.ShapeDtypeStruct((steps, tp_count, 3, piece, LANES), wide),
        ],
        in_specs=[smem] * 3 + [hbm] * 4,
        out_specs=[vmem, hbm],
        scratch_shapes=[
            pltpu.VMEM((STAGES, tp_count * 3 * piece, LANES), wide),
            pltpu.VMEM((SENDS, fsdp_count, 3 * pair, LANES), wide),
        ]
        + [pltpu.VMEM((fsdp_count, 3 * pair, LANES), wide)] * ARRIVALS
        + [
            pltpu.VMEM((steps, block_rows, LANES), grad.dtype),
            pltpu.VMEM((1, LANES), wide),
            pltpu.VMEM((1, LANES), wide),
            pltpu.VMEM((tp_count, 1, LANES), wide),
            pltpu.VMEM((fsdp_count, 1, LANES), wide),
            pltpu.VMEM((1, LANES), wide),
            dma((steps,)),
            dma((steps,)),
            dma((STAGES,)),
            dma((SENDS,)),
            dma((steps,)),
            dma,
            dma((4,)),
        ],
        compiler_params=pltpu.CompilerParams(
            has_side_effects=True, vmem_limit_bytes=22 << 20
        ),
        name="restore",
    )(send_idx, place_idx, fixes, saved_master, saved_first, saved_second, grad)

    out = jax.ShapeDtypeStruct((block_rows, columns), wide)
    return tuple(
        pl.pallas_call(
            drain_kernel,
            out_shape=[out] * 4,
            in_specs=[pl.BlockSpec(memory_space=pl.ANY)],
            out_specs=[hbm] * 4,
            scratch_shapes=[dma((4, steps))],
            compiler_params=pltpu.CompilerParams(vmem_limit_bytes=1 << 20),
            name="drain",
        )(held)
    )


def solution(mesh):
    in_specs = (
        P(("fsdp", "tp"), None),
        P(("fsdp", "tp"), None),
        P(("fsdp", "tp"), None),
        P("fsdp", "tp"),
        P(),
        P(),
    )
    out_specs = (P("fsdp", "tp"), P("fsdp", "tp"), P("fsdp", "tp"), P("fsdp", "tp"))

    def whole(saved_master, saved_first, saved_second, grad, row_target, step):
        def body(*args):
            return per_device(grad.shape[0] * grad.shape[1], *args)

        return jax.shard_map(
            body, mesh=mesh, in_specs=in_specs, out_specs=out_specs, check_vma=False
        )(saved_master, saved_first, saved_second, grad, row_target, step)

    return whole
```

time: 830 us -> 752 us (0.906)
  Pallas kernels: 39.2 us -> 731 us
  waiting for transfers between devices: 404 us -> 0 us
  local copies, waits for them, and re-layouts: 132 us -> 0.7 us
  starting transfers between devices: 123 us -> 0 us
  blocking collectives: 64.5 us -> 0 us
  other arithmetic: 53.4 us -> 14.7 us
    pallas_call x6 -> x2, Pallas kernels: 39.2 us -> 731 us  [the longest x1 717 us: per_device(): pl.pallas_call(kernel, out_shape=[pltpu.VMEM((4, steps, block_rows, LANES...]
    ppermute x6 -> x0, waiting for transfers between devices: 272 us -> none  [per_device(): pieces.append(lax.ppermute(outgoing, 'tp', pairs))]
    all_to_all x6 -> x0, waiting for transfers between devices: 132 us -> none  [per_device(): lax.all_to_all(gathered, 'fsdp', split_axis=0, concat_axis=0, tiled=True)]
    all_to_all x6 -> x0, starting transfers between devices: 116 us -> none  [per_device(): lax.all_to_all(gathered, 'fsdp', split_axis=0, concat_axis=0, tiled=True)]
    gather x12 -> x0, local copies, waits for them, and re-layouts: 105 us -> none  [the longest x6 52.7 us: per_device(): gathered = jnp.concatenate(pieces, axis=0)[send_local]]
    unnamed x1 -> x0, blocking collectives: 64.5 us -> none
    slice x8 -> x0, local copies, waits for them, and re-layouts: 25.1 us -> none  [part_of(): x[:, t * columns + begin:t * columns + end]]
    select_n x7 -> x1, other arithmetic: 18.7 us -> 0.01 us  [per_device(): jnp.argsort(sort_keys, stable=True)[:block_rows].astype(jnp.int32)]
  transfers between devices with their start and end apart: 12 -> 0, of which waited for: 8 -> 0; matrix products, arithmetic and copies ran while one was open for 20% -> 0% of each run, Pallas kernels for 4% -> 0%
where the time goes in v1:
time: 752 us; the launch traced here: 748 us
  Pallas kernels  731 us (97%)
  other arithmetic  14.7 us (2%)
    pallas_call x1, Pallas kernels, per_device(): pl.pallas_call(kernel, out_shape=[pltpu.VMEM((4, steps, block_rows, LANES...  717 us

profile of v1, /device:TPU:1, one launch (start us, length us, event | category | flops | bytes accessed | tf_op | source)
XLA Modules:
  0.0 747.7 jit_solution(16068176012169634229)
XLA Ops:
  1.4 0.6 pad_maximum_fusion.refs_2_
  2.0 0.7 dynamic_slice.3
  2.6 4.4 sort.34
  7.0 0.9 fusion.4
  7.9 7.8 %sort.35 = (s32[16384]{0:T(1024)}, s32[16384]{0:T(1024)S(1)}) sort(s32[16384]{0:T(1024)S(1)} %fusion.4, s32[16384]{0:T(1024)S(1)} %iota.16), dimensions={0}, to_apply=%region_1.2 | sort | flops 229376 | bytes 262144 | tf_op jit(solution)/shard_map/jit(argsort)/sort | solution.py:338
  15.7 0.5 convert_reduce_fusion
  16.2 0.6 fusion.6
  16.8 716.9 %restore.1 = (f32[4,20,1024,128]{3,2,1,0:T(8,128)S(1)}, f32[20,2,3,512,128]{4,3,2,1,0:T(8,128)}) custom-call(s32[1024]{0:T(1024)} %get-tuple-element.10.refs_0_, s32[1024]{0:T(1024)} %get-tuple-element.11.refs_1_, f32[2]{0:T(128)} %pad_maximum_fusion.refs_2_, f32[512,5120]{1,0:T(8,128)} %refs_3_.1, f32[512,5120]{1,0:T(8,128)} %refs_4_.1, ...), custom_call_target="tpu_custom_call" | custom-call | tf_op jit(solution)/shard_map/restore/pallas_call | solution.py:359
  733.7 14.1 %drain.1 = (f32[1024,2560]{1,0:T(8,128)}, f32[1024,2560]{1,0:T(8,128)}, f32[1024,2560]{1,0:T(8,128)}, f32[1024,2560]{1,0:T(8,128)}) custom-call(f32[4,20,1024,128]{3,2,1,0:T(8,128)S(1)} %get-tuple-element.9.held), custom_call_target="tpu_custom_call" | custom-call | tf_op jit(solution)/shard_map/drain/pallas_call | solution.py:395
  (3 shorter events, 0.0 us)

commit v2 on v1

v2 whole, which is shorter than its diff:
```python
import math

import jax
import jax.numpy as jnp
from jax import lax
from jax.experimental import pallas as pl
from jax.experimental.pallas import tpu as pltpu
from jax.sharding import PartitionSpec as P

beta_one = 0.9
beta_two = 0.95
epsilon = 1e-08
learn_rate = 0.001
weight_decay = 0.1

LANES = 128
SENDS = 2
ARRIVALS = 3
MESH = pl.DeviceIdType.MESH


def partner_steps(count):
    bits = count.bit_length() - 1
    if 1 << bits != count:
        return list(range(1, count))
    return [int(format(i, f"0{bits}b")[::-1], 2) for i in range(1, count)]


def restore_kernel(count, entries, *refs):
    tp_count, fsdp_count = count
    send_idx, place_idx, fixes, master_ref, first_ref, second_ref, grad_ref = refs[:7]
    out, landed = refs[7:9]
    stages, send = refs[9:12], refs[12]
    arrivals = [refs[13 + 3 * i : 16 + 3 * i] for i in range(ARRIVALS)]
    grad, partial, partial_row, from_tp, from_fsdp, scale_ref = refs[-13:-7]
    tp_sent, tp_landed, staged, sent, arrived, grad_sem, partial_sems = refs[-7:]
    f, t = lax.axis_index("fsdp"), lax.axis_index("tp")
    saved = (master_ref, first_ref, second_ref)
    steps, block_rows = out.shape[1], out.shape[2]
    columns = steps * LANES
    piece = master_ref.shape[0]
    pair = block_rows // fsdp_count
    power = fsdp_count & (fsdp_count - 1) == 0
    flat = pair % 8 == 0

    def along_tp(d):
        return lax.rem(t + d, tp_count)

    def along_fsdp(d):
        return jnp.bitwise_xor(f, d) if power else lax.rem(f + d, fsdp_count)

    def unit(ref, half, s):
        return ref.at[:, pl.ds(pl.multiple_of(half * columns + s * LANES, LANES), LANES)]

    def tp_start(s, x):
        for d in range(1, tp_count):
            peer = along_tp(d)
            pltpu.make_async_remote_copy(
                src_ref=unit(saved[x], peer, s),
                dst_ref=landed.at[s, x, t],
                send_sem=tp_sent.at[s, x],
                recv_sem=tp_landed.at[s, x],
                device_id=(f, peer),
                device_id_type=MESH,
            ).start()

    def tp_wait(s, x, sem):
        if tp_count > 1:
            whole = landed.at[s, x, pl.ds(0, tp_count - 1)]
            pltpu.make_async_copy(whole, whole, sem.at[s, x]).wait()

    def stage_start(s, x):
        for d in range(tp_count):
            half = along_tp(d)
            rows = pl.ds(pl.multiple_of(half * piece, 8), piece)
            source = unit(saved[x], t, s) if d == 0 else landed.at[s, x, half]
            pltpu.make_async_copy(source, stages[x].at[rows], staged.at[x]).start()

    def stage_wait(x):
        pltpu.make_async_copy(stages[x], stages[x], staged.at[x]).wait()

    def with_arrival(s, x, body):
        for i, held in enumerate(arrivals):
            pl.when(lax.rem(s, ARRIVALS) == i)(lambda recv=held[x]: body(s, x, recv))

    def block_of(recv, b):
        return pl.ds(pl.multiple_of(b * pair, 8), pair) if flat else b

    def send_start(s, x, recv):
        slot = lax.rem(s, SENDS)
        recv[block_of(recv, f)] = send[slot, x, f]
        for d in partner_steps(fsdp_count):
            peer = along_fsdp(d)
            pltpu.make_async_remote_copy(
                src_ref=send.at[slot, x, peer],
                dst_ref=recv.at[block_of(recv, f)],
                send_sem=sent.at[slot, x],
                recv_sem=arrived.at[s, x],
                device_id=(peer, t),
                device_id_type=MESH,
            ).start()

    def exchanged():
        return send.at[0, 0, pl.ds(0, fsdp_count - 1)]

    def send_wait(s, x):
        pltpu.make_async_copy(exchanged(), exchanged(), sent.at[lax.rem(s, SENDS), x]).wait()

    def recv_wait(s, x):
        pltpu.make_async_copy(exchanged(), exchanged(), arrived.at[s, x]).wait()

    run = math.gcd(pair, 8)

    def gather(s, x):
        slot = lax.rem(s, SENDS)

        def one_block(b, carry):
            def one_run(k, carry):
                for u in range(run):
                    row = send_idx[b * pair + k * run + u]
                    send[slot, x, b, pl.ds(k * run + u, 1), :] = stages[x][pl.ds(row, 1), :]
                return carry

            return lax.fori_loop(0, pair // run, one_run, carry)

        lax.fori_loop(0, fsdp_count, one_block, 0)

    def place(s, x, recv):
        def one_run(k, carry):
            for u in range(8):
                index = place_idx[k * 8 + u]
                if flat:
                    row = recv[pl.ds(index, 1), :]
                else:
                    row = recv[index // pair, pl.ds(index % pair, 1), :]
                out[x, s, pl.ds(k * 8 + u, 1), :] = row
            return carry

        lax.fori_loop(0, block_rows // 8, one_run, 0)

    tile = math.gcd(block_rows, 64)

    def adam(s):
        scale = scale_ref[...]
        first_fix, second_fix = fixes[0], fixes[1]

        def one_tile(k, carry):
            rows = pl.ds(pl.multiple_of(k * tile, tile), tile)
            clipped = scale * grad[s, rows, :].astype(jnp.float32)
            master = out[0, s, rows, :]
            first_new = beta_one * out[1, s, rows, :] + (1.0 - beta_one) * clipped
            second_new = beta_two * out[2, s, rows, :] + (1.0 - beta_two) * clipped * clipped
            first_hat = first_new / first_fix
            second_hat = second_new / second_fix
            direction = first_hat / (jnp.sqrt(second_hat) + epsilon) + weight_decay * master
            out[0, s, rows, :] = master - learn_rate * direction
            out[1, s, rows, :] = first_new
            out[2, s, rows, :] = second_new
            out[3, s, rows, :] = direction
            return carry

        lax.fori_loop(0, block_rows // tile, one_tile, 0)

    def square_sum():
        def one_unit(s, total):
            def one_tile(k, total):
                rows = pl.ds(pl.multiple_of(k * tile, tile), tile)
                wide = grad[s, rows, :].astype(jnp.float32)
                return total + wide * wide

            return lax.fori_loop(0, block_rows // tile, one_tile, total)

        total = lax.fori_loop(0, steps, one_unit, jnp.zeros((tile, LANES), jnp.float32))
        return jnp.sum(total, axis=0, keepdims=True)

    def partial_copies(which):
        if which == 0:
            peers = [(f, along_tp(d)) for d in range(1, tp_count)]
            source, target = partial, from_tp.at[t]
        else:
            peers = [(along_fsdp(d), t) for d in partner_steps(fsdp_count)]
            source, target = partial_row, from_fsdp.at[f]
        return [
            pltpu.make_async_remote_copy(
                src_ref=source,
                dst_ref=target,
                send_sem=partial_sems.at[2 * which],
                recv_sem=partial_sems.at[2 * which + 1],
                device_id=peer,
                device_id_type=MESH,
            )
            for peer in peers
        ]

    def partial_wait(which, side):
        held = (from_tp, from_fsdp)[which]
        members = (tp_count, fsdp_count)[which]
        if members > 1:
            whole = held.at[pl.ds(0, members - 1)]
            pltpu.make_async_copy(whole, whole, partial_sems.at[2 * which + side]).wait()

    def summed(held, members):
        total = held[0]
        for i in range(1, members):
            total = total + held[i]
        return total

    def grad_copy(s):
        return pltpu.make_async_copy(unit(grad_ref, 0, s), grad.at[s], grad_sem)

    def over_steps(body):
        lax.fori_loop(0, steps, lambda s, carry: (body(s), carry)[1], 0)

    for x in range(3):
        tp_start(0, x)
    over_steps(lambda s: grad_copy(s).start())
    tp_wait(0, 0, tp_landed)
    stage_start(0, 0)

    def begin_total():
        pltpu.make_async_copy(grad, grad, grad_sem).wait()
        own = square_sum()
        partial[...] = own
        from_tp[t] = own
        for copy in partial_copies(0):
            copy.start()

    def spread_total():
        partial_wait(0, 1)
        row = summed(from_tp, tp_count)
        partial_row[...] = row
        from_fsdp[f] = row
        for copy in partial_copies(1):
            copy.start()

    def end_total():
        partial_wait(1, 1)
        total = jnp.sum(summed(from_fsdp, fsdp_count), axis=1, keepdims=True)
        scale = jnp.minimum(1.0, math.sqrt(entries) / jnp.sqrt(total))
        scale_ref[...] = jnp.broadcast_to(scale, scale_ref.shape)

    def step(s, carry):
        for x in range(3):

            @pl.when(s < steps)
            def _():
                stage_wait(x)
                pl.when(s >= SENDS)(lambda: send_wait(s - SENDS, x))
                gather(s, x)
                with_arrival(s, x, send_start)
                pl.when(s + 1 < steps)(lambda: tp_start(s + 1, x))
                if x == 0:
                    pl.when(s == 0)(begin_total)
                if x == 2:
                    pl.when(s == 0)(spread_total)
                after, y = (s, x + 1) if x < 2 else (s + 1, 0)

                @pl.when(after < steps)
                def _():
                    tp_wait(after, y, tp_landed)
                    stage_start(after, y)

            @pl.when(s >= 1)
            def _():
                recv_wait(s - 1, x)
                with_arrival(s - 1, x, place)

        @pl.when(s >= 1)
        def _():
            pl.when(s == 1)(end_total)
            adam(s - 1)

        return carry

    lax.fori_loop(0, steps + 1, step, 0)
    for x in range(3):
        for s in range(max(0, steps - SENDS), steps):
            send_wait(s, x)
        over_steps(lambda s: tp_wait(s, x, tp_sent))
    partial_wait(0, 0)
    partial_wait(1, 0)


def drain_kernel(held, *refs):
    outs, sem = refs[:-1], refs[-1]
    copies = [
        pltpu.make_async_copy(
            held.at[i, u], out.at[:, u * LANES : (u + 1) * LANES], sem.at[i, u]
        )
        for i, out in enumerate(outs)
        for u in range(held.shape[1])
    ]
    for copy in copies:
        copy.start()
    for copy in copies:
        copy.wait()


def per_device(entries, saved_master, saved_first, saved_second, grad, row_target, step):
    tp_count, fsdp_count = lax.axis_size("tp"), lax.axis_size("fsdp")
    block_index = lax.axis_index("fsdp")
    block_rows, columns = grad.shape
    piece = saved_master.shape[0]
    all_rows = row_target.shape[0]
    pair = block_rows // fsdp_count
    steps = columns // LANES

    mine = lax.dynamic_slice_in_dim(row_target, block_index * block_rows, block_rows)
    send_order = jnp.argsort(mine, stable=True).astype(jnp.int32)
    send_idx = send_order

    in_block = row_target // block_rows == block_index
    sort_keys = jnp.where(in_block, row_target, all_rows)
    source_block = jnp.argsort(sort_keys, stable=True)[:block_rows].astype(jnp.int32) // block_rows
    local = jnp.arange(block_rows, dtype=jnp.int32)
    before = (source_block[None, :] == source_block[:, None]) & (local[None, :] < local[:, None])
    place_idx = source_block * pair + jnp.sum(before.astype(jnp.int32), axis=1)

    taken = step[0].astype(jnp.float32)
    fixes = jnp.stack(
        [
            1.0 - jnp.power(jnp.float32(beta_one), taken),
            1.0 - jnp.power(jnp.float32(beta_two), taken),
        ]
    )

    def kernel(*refs):
        restore_kernel((tp_count, fsdp_count), entries, *refs)

    smem = pl.BlockSpec(memory_space=pltpu.SMEM)
    hbm = pl.BlockSpec(memory_space=pltpu.HBM)
    vmem = pl.BlockSpec(memory_space=pltpu.VMEM)
    dma = pltpu.SemaphoreType.DMA
    wide = jnp.float32
    blocks = (block_rows,) if pair % 8 == 0 else (fsdp_count, pair)
    arrival = pltpu.VMEM((*blocks, LANES), wide)
    held, _ = pl.pallas_call(
        kernel,
        out_shape=[
            pltpu.VMEM((4, steps, block_rows, LANES), wide),
            jax.ShapeDtypeStruct((steps, 3, tp_count, piece, LANES), wide),
        ],
        in_specs=[smem] * 3 + [hbm] * 4,
        out_specs=[vmem, hbm],
        scratch_shapes=[
            pltpu.VMEM((tp_count * piece, LANES), wide),
            pltpu.VMEM((tp_count * piece, LANES), wide),
            pltpu.VMEM((tp_count * piece, LANES), wide),
            pltpu.VMEM((SENDS, 3, fsdp_count, pair, LANES), wide),
        ]
        + [arrival] * (3 * ARRIVALS)
        + [
            pltpu.VMEM((steps, block_rows, LANES), grad.dtype),
            pltpu.VMEM((1, LANES), wide),
            pltpu.VMEM((1, LANES), wide),
            pltpu.VMEM((tp_count, 1, LANES), wide),
            pltpu.VMEM((fsdp_count, 1, LANES), wide),
            pltpu.VMEM((1, LANES), wide),
            dma((steps, 3)),
            dma((steps, 3)),
            dma((3,)),
            dma((SENDS, 3)),
            dma((steps, 3)),
            dma,
            dma((4,)),
        ],
        compiler_params=pltpu.CompilerParams(
            has_side_effects=True, vmem_limit_bytes=22 << 20
        ),
        name="restore",
    )(send_idx, place_idx, fixes, saved_master, saved_first, saved_second, grad)

    out = jax.ShapeDtypeStruct((block_rows, columns), wide)
    return tuple(
        pl.pallas_call(
            drain_kernel,
            out_shape=[out] * 4,
            in_specs=[pl.BlockSpec(memory_space=pl.ANY)],
            out_specs=[hbm] * 4,
            scratch_shapes=[dma((4, steps))],
            compiler_params=pltpu.CompilerParams(vmem_limit_bytes=1 << 20),
            name="drain",
        )(held)
    )


def solution(mesh):
    in_specs = (
        P(("fsdp", "tp"), None),
        P(("fsdp", "tp"), None),
        P(("fsdp", "tp"), None),
        P("fsdp", "tp"),
        P(),
        P(),
    )
    out_specs = (P("fsdp", "tp"), P("fsdp", "tp"), P("fsdp", "tp"), P("fsdp", "tp"))

    def whole(saved_master, saved_first, saved_second, grad, row_target, step):
        def body(*args):
            return per_device(grad.shape[0] * grad.shape[1], *args)

        return jax.shard_map(
            body, mesh=mesh, in_specs=in_specs, out_specs=out_specs, check_vma=False
        )(saved_master, saved_first, saved_second, grad, row_target, step)

    return whole
```

time: 752 us -> 732 us (0.973)
  Pallas kernels: 731 us -> 715 us
    pallas_call x1, Pallas kernels: 717 us -> 701 us  [per_device(): pl.pallas_call(kernel, out_shape=[pltpu.VMEM((4, steps, block_rows, LANES...]
where the time goes in v2:
time: 732 us; the launch traced here: 731 us
  Pallas kernels  715 us (98%)
  other arithmetic  14.7 us (2%)
    pallas_call x1, Pallas kernels, per_device(): pl.pallas_call(kernel, out_shape=[pltpu.VMEM((4, steps, block_rows, LANES...  701 us

profile of v2, /device:TPU:1, one launch (start us, length us, event | category | flops | bytes accessed | tf_op | source)
XLA Modules:
  0.0 731.4 jit_solution(643787793555197119)
XLA Ops:
  1.4 0.6 pad_maximum_fusion.refs_2_
  2.0 0.7 dynamic_slice.3
  2.6 4.4 sort.34
  7.0 0.9 fusion.4
  7.9 7.8 %sort.35 = (s32[16384]{0:T(1024)}, s32[16384]{0:T(1024)S(1)}) sort(s32[16384]{0:T(1024)S(1)} %fusion.4, s32[16384]{0:T(1024)S(1)} %iota.16), dimensions={0}, to_apply=%region_1.2 | sort | flops 229376 | bytes 262144 | tf_op jit(solution)/shard_map/jit(argsort)/sort | solution.py:314
  15.7 0.5 convert_reduce_fusion
  16.2 0.6 multiply_add_fusion.refs_1_
  16.8 700.5 %restore.1 = (f32[4,20,1024,128]{3,2,1,0:T(8,128)S(1)}, f32[20,3,2,512,128]{4,3,2,1,0:T(8,128)}) custom-call(s32[1024]{0:T(1024)} %get-tuple-element.7.refs_0_, s32[1024]{0:T(1024)} %multiply_add_fusion.refs_1_, f32[2]{0:T(128)} %pad_maximum_fusion.refs_2_, f32[512,5120]{1,0:T(8,128)} %refs_3_.1, f32[512,5120]{1,0:T(8,128)} %refs_4_.1, f32[512,5120]{1,0:T(8,128)} %refs_5_.1, ...), custom_call_target="tpu_custom_call" | custom-call | tf_op jit(solution)/shard_map/restore/pallas_call | solution.py:337
  717.4 14.1 %drain.1 = (f32[1024,2560]{1,0:T(8,128)}, f32[1024,2560]{1,0:T(8,128)}, f32[1024,2560]{1,0:T(8,128)}, f32[1024,2560]{1,0:T(8,128)}) custom-call(f32[4,20,1024,128]{3,2,1,0:T(8,128)S(1)} %get-tuple-element.9.held), custom_call_target="tpu_custom_call" | custom-call | tf_op jit(solution)/shard_map/drain/pallas_call | solution.py:375
  (3 shorter events, 0.0 us)

commit v3 on v2

--- a/solution.py
+++ b/solution.py
@@ -16,6 +16,7 @@
 LANES = 128
 SENDS = 2
 ARRIVALS = 3
+UNROLL = 32
 MESH = pl.DeviceIdType.MESH
 
 
@@ -28,10 +29,11 @@
 
 def restore_kernel(count, entries, *refs):
     tp_count, fsdp_count = count
-    send_idx, place_idx, fixes, master_ref, first_ref, second_ref, grad_ref = refs[:7]
-    out, landed = refs[7:9]
-    stages, send = refs[9:12], refs[12]
-    arrivals = [refs[13 + 3 * i : 16 + 3 * i] for i in range(ARRIVALS)]
+    step_ref, target_ref, master_ref, first_ref, second_ref, grad_ref = refs[:6]
+    out, landed = refs[6:8]
+    send_idx, place_idx, send_table, place_table, spread, table_sem = refs[8:14]
+    stages, send = refs[14:17], refs[17]
+    arrivals = [refs[18 + 3 * i : 21 + 3 * i] for i in range(ARRIVALS)]
     grad, partial, partial_row, from_tp, from_fsdp, scale_ref = refs[-13:-7]
     tp_sent, tp_landed, staged, sent, arrived, grad_sem, partial_sems = refs[-7:]
     f, t = lax.axis_index("fsdp"), lax.axis_index("tp")
@@ -52,12 +54,15 @@
     def unit(ref, half, s):
         return ref.at[:, pl.ds(pl.multiple_of(half * columns + s * LANES, LANES), LANES)]
 
-    def tp_start(s, x):
+    def half_rows(half):
+        return pl.ds(pl.multiple_of(half * piece, 8), piece)
+
+    def tp_start(s, x, first=False):
         for d in range(1, tp_count):
             peer = along_tp(d)
             pltpu.make_async_remote_copy(
                 src_ref=unit(saved[x], peer, s),
-                dst_ref=landed.at[s, x, t],
+                dst_ref=stages[x].at[half_rows(t)] if first else landed.at[s, x, t],
                 send_sem=tp_sent.at[s, x],
                 recv_sem=tp_landed.at[s, x],
                 device_id=(f, peer),
@@ -69,15 +74,20 @@
             whole = landed.at[s, x, pl.ds(0, tp_count - 1)]
             pltpu.make_async_copy(whole, whole, sem.at[s, x]).wait()
 
+    def stage_own(s, x):
+        return pltpu.make_async_copy(unit(saved[x], t, s), stages[x].at[half_rows(t)], staged.at[x])
+
     def stage_start(s, x):
-        for d in range(tp_count):
+        stage_own(s, x).start()
+        for d in range(1, tp_count):
             half = along_tp(d)
-            rows = pl.ds(pl.multiple_of(half * piece, 8), piece)
-            source = unit(saved[x], t, s) if d == 0 else landed.at[s, x, half]
-            pltpu.make_async_copy(source, stages[x].at[rows], staged.at[x]).start()
-
-    def stage_wait(x):
-        pltpu.make_async_copy(stages[x], stages[x], staged.at[x]).wait()
+            source = landed.at[s, x, half]
+            pltpu.make_async_copy(source, stages[x].at[half_rows(half)], staged.at[x]).start()
+
+    def stage_wait(s, x):
+        pl.when(s == 0)(lambda: (stage_own(s, x).wait(), tp_wait(s, x, tp_landed))[1])
+        whole = stages[x]
+        pl.when(s > 0)(lambda: pltpu.make_async_copy(whole, whole, staged.at[x]).wait())
 
     def with_arrival(s, x, body):
         for i, held in enumerate(arrivals):
@@ -109,15 +119,86 @@
     def recv_wait(s, x):
         pltpu.make_async_copy(exchanged(), exchanged(), arrived.at[s, x]).wait()
 
-    run = math.gcd(pair, 8)
+    lines = block_rows // LANES
+    square = (LANES, LANES)
+    lane = lax.broadcasted_iota(jnp.int32, square, 1)
+    sublane = lax.broadcasted_iota(jnp.int32, square, 0)
+
+    def across(column):
+        return jnp.broadcast_to(column, square)
+
+    def turned(row):
+        return jnp.transpose(across(row))
+
+    def ones_where(mask):
+        return jnp.where(mask, 1, 0)
+
+    def inside(index):
+        return jnp.clip(index, 0, block_rows - 1)
+
+    def to_scalars(table, idx):
+        copy = pltpu.make_async_copy(table, idx, table_sem)
+        copy.start()
+        copy.wait()
+
+    def fill_send_idx():
+        mine = [target_ref[pl.ds(f * lines + c, 1), :] for c in range(lines)]
+        for c in range(lines):
+            column, smaller = turned(mine[c]), jnp.zeros(square, jnp.int32)
+            for row in mine:
+                smaller = smaller + ones_where(row < column)
+            spread[c] = across(jnp.sum(smaller, axis=1, keepdims=True))
+        for c in range(lines):
+            source = jnp.zeros(square, jnp.int32)
+            for d in range(lines):
+                source = source + jnp.where(spread[d] == c * LANES + lane, d * LANES + sublane, 0)
+            send_table[pl.ds(c, 1), :] = inside(jnp.sum(source, axis=0, keepdims=True))
+        to_scalars(send_table, send_idx)
+
+    def fill_place_idx():
+        def one_line(c, carry):
+            wanted = f * block_rows + c * LANES + sublane
+
+            def one_row(k, block):
+                return block + jnp.where(target_ref[pl.ds(k, 1), :] == wanted, k // lines, 0)
+
+            block = lax.fori_loop(
+                0, target_ref.shape[0], one_row, jnp.zeros(square, jnp.int32), unroll=4
+            )
+            spread[c] = across(jnp.sum(block, axis=1, keepdims=True))
+            place_table[pl.ds(c, 1), :] = jnp.transpose(spread[c])[:1]
+            return carry
+
+        lax.fori_loop(0, lines, one_line, 0)
+        blocks = [place_table[pl.ds(c, 1), :] for c in range(lines)]
+        for c in range(lines):
+            column = spread[c]
+            earlier = ones_where((blocks[c] == column) & (lane < sublane))
+            for d in range(c):
+                earlier = earlier + ones_where(blocks[d] == column)
+            rank = jnp.sum(earlier, axis=1, keepdims=True)
+            place_table[pl.ds(c, 1), :] = inside(jnp.transpose(column * pair + across(rank))[:1])
+        to_scalars(place_table, place_idx)
+
+    def power_of(base):
+        def one_bit(i, carry):
+            result, factor = carry
+            odd = lax.shift_right_logical(step_ref[0], i) & 1
+            return jnp.where(odd == 1, result * factor, result), factor * factor
+
+        return lax.fori_loop(0, 31, one_bit, (jnp.float32(1.0), jnp.float32(base)))[0]
+
+    run = math.gcd(pair, UNROLL)
 
     def gather(s, x):
         slot = lax.rem(s, SENDS)
 
         def one_block(b, carry):
             def one_run(k, carry):
+                at = b * pair + k * run
+                line, column = at // LANES, at % LANES
                 for u in range(run):
-                    row = send_idx[b * pair + k * run + u]
+                    row = send_idx[line, column + u]
                     send[slot, x, b, pl.ds(k * run + u, 1), :] = stages[x][pl.ds(row, 1), :]
                 return carry
 
@@ -126,23 +207,27 @@
         lax.fori_loop(0, fsdp_count, one_block, 0)
 
     def place(s, x, recv):
-        def one_run(k, carry):
-            for u in range(8):
-                index = place_idx[k * 8 + u]
-                if flat:
-                    row = recv[pl.ds(index, 1), :]
-                else:
-                    row = recv[index // pair, pl.ds(index % pair, 1), :]
-                out[x, s, pl.ds(k * 8 + u, 1), :] = row
-            return carry
-
-        lax.fori_loop(0, block_rows // 8, one_run, 0)
+        def one_line(c, carry):
+            def one_run(k, carry):
+                for u in range(UNROLL):
+                    index = place_idx[c, k * UNROLL + u]
+                    if flat:
+                        row = recv[pl.ds(index, 1), :]
+                    else:
+                        row = recv[index // pair, pl.ds(index % pair, 1), :]
+                    out[x, s, pl.ds(c * LANES + k * UNROLL + u, 1), :] = row
+                return carry
+
+            return lax.fori_loop(0, LANES // UNROLL, one_run, carry)
+
+        lax.fori_loop(0, lines, one_line, 0)
 
     tile = math.gcd(block_rows, 64)
 
     def adam(s):
         scale = scale_ref[...]
-        first_fix, second_fix = fixes[0], fixes[1]
+        first_fix = 1.0 - power_of(beta_one)
+        second_fix = 1.0 - power_of(beta_two)
 
         def one_tile(k, carry):
             rows = pl.ds(pl.multiple_of(k * tile, tile), tile)
@@ -212,10 +297,10 @@
         lax.fori_loop(0, steps, lambda s, carry: (body(s), carry)[1], 0)
 
     for x in range(3):
-        tp_start(0, x)
+        tp_start(0, x, True)
+        stage_own(0, x).start()
     over_steps(lambda s: grad_copy(s).start())
-    tp_wait(0, 0, tp_landed)
-    stage_start(0, 0)
+    fill_send_idx()
 
     def begin_total():
         pltpu.make_async_copy(grad, grad, grad_sem).wait()
@@ -244,18 +329,20 @@
 
             @pl.when(s < steps)
             def _():
-                stage_wait(x)
+                stage_wait(s, x)
                 pl.when(s >= SENDS)(lambda: send_wait(s - SENDS, x))
                 gather(s, x)
                 with_arrival(s, x, send_start)
                 pl.when(s + 1 < steps)(lambda: tp_start(s + 1, x))
                 if x == 0:
                     pl.when(s == 0)(begin_total)
+                if x == 1:
+                    pl.when(s == 0)(fill_place_idx)
                 if x == 2:
                     pl.when(s == 0)(spread_total)
                 after, y = (s, x + 1) if x < 2 else (s + 1, 0)
 
-                @pl.when(after < steps)
+                @pl.when((after > 0) & (after < steps))
                 def _():
                     tp_wait(after, y, tp_landed)
                     stage_start(after, y)
@@ -298,31 +385,11 @@
 
 def per_device(entries, saved_master, saved_first, saved_second, grad, row_target, step):
     tp_count, fsdp_count = lax.axis_size("tp"), lax.axis_size("fsdp")
-    block_index = lax.axis_index("fsdp")
     block_rows, columns = grad.shape
     piece = saved_master.shape[0]
-    all_rows = row_target.shape[0]
+    lines = block_rows // LANES
     pair = block_rows // fsdp_count
     steps = columns // LANES
-
-    mine = lax.dynamic_slice_in_dim(row_target, block_index * block_rows, block_rows)
-    send_order = jnp.argsort(mine, stable=True).astype(jnp.int32)
-    send_idx = send_order
-
-    in_block = row_target // block_rows == block_index
-    sort_keys = jnp.where(in_block, row_target, all_rows)
-    source_block = jnp.argsort(sort_keys, stable=True)[:block_rows].astype(jnp.int32) // block_rows
-    local = jnp.arange(block_rows, dtype=jnp.int32)
-    before = (source_block[None, :] == source_block[:, None]) & (local[None, :] < local[:, None])
-    place_idx = source_block * pair + jnp.sum(before.astype(jnp.int32), axis=1)
-
-    taken = step[0].astype(jnp.float32)
-    fixes = jnp.stack(
-        [
-            1.0 - jnp.power(jnp.float32(beta_one), taken),
-            1.0 - jnp.power(jnp.float32(beta_two), taken),
-        ]
-    )
 
     def kernel(*refs):
         restore_kernel((tp_count, fsdp_count), entries, *refs)
@@ -340,9 +407,15 @@
             pltpu.VMEM((4, steps, block_rows, LANES), wide),
             jax.ShapeDtypeStruct((steps, 3, tp_count, piece, LANES), wide),
         ],
-        in_specs=[smem] * 3 + [hbm] * 4,
+        in_specs=[smem, vmem] + [hbm] * 4,
         out_specs=[vmem, hbm],
         scratch_shapes=[
+            pltpu.SMEM((lines, LANES), jnp.int32),
+            pltpu.SMEM((lines, LANES), jnp.int32),
+            pltpu.VMEM((lines, LANES), jnp.int32),
+            pltpu.VMEM((lines, LANES), jnp.int32),
+            pltpu.VMEM((lines, LANES, LANES), jnp.int32),
+            dma,
             pltpu.VMEM((tp_count * piece, LANES), wide),
             pltpu.VMEM((tp_count * piece, LANES), wide),
             pltpu.VMEM((tp_count * piece, LANES), wide),
@@ -368,7 +441,7 @@
             has_side_effects=True, vmem_limit_bytes=22 << 20
         ),
         name="restore",
-    )(send_idx, place_idx, fixes, saved_master, saved_first, saved_second, grad)
+    )(step, row_target.reshape(-1, LANES), saved_master, saved_first, saved_second, grad)
 
     out = jax.ShapeDtypeStruct((block_rows, columns), wide)
     return tuple(

time: 732 us -> 718 us (0.981)
  other arithmetic: 14.7 us -> 0 us
    sort x2 -> x0, other arithmetic: 12.1 us -> none  [the longest x1 7.75 us: per_device(): jnp.argsort(sort_keys, stable=True)[:block_rows].astype(jnp.int32)]
where the time goes in v3:
time: 718 us; the launch traced here: 717 us
  Pallas kernels  716 us (100%)
    pallas_call x1, Pallas kernels, per_device(): pl.pallas_call(kernel, out_shape=[pltpu.VMEM((4, steps, block_rows, LANES...  702 us

profile of v3, /device:TPU:1, one launch (start us, length us, event | category | flops | bytes accessed | tf_op | source)
XLA Modules:
  0.0 717.4 jit_solution(15482584973880849060)
XLA Ops:
  1.3 702.0 %restore.1 = (f32[4,20,1024,128]{3,2,1,0:T(8,128)S(1)}, f32[20,3,2,512,128]{4,3,2,1,0:T(8,128)}) custom-call(s32[1]{0:T(128)S(6)} %copy.10.refs_0_, s32[128,128]{1,0:T(8,128)} %bitcast.1, f32[512,5120]{1,0:T(8,128)} %refs_2_.1, f32[512,5120]{1,0:T(8,128)} %refs_3_.1, f32[512,5120]{1,0:T(8,128)} %refs_4_.1, bf16[1024,2560]{1,0:T(8,128)(2,1)} %refs_5_.1), custom_call_target="tpu_custom_call" | custom-call | tf_op jit(solution)/shard_map/restore/pallas_call | solution.py:404
  703.3 14.1 %drain.1 = (f32[1024,2560]{1,0:T(8,128)}, f32[1024,2560]{1,0:T(8,128)}, f32[1024,2560]{1,0:T(8,128)}, f32[1024,2560]{1,0:T(8,128)}) custom-call(f32[4,20,1024,128]{3,2,1,0:T(8,128)S(1)} %get-tuple-element.5.held), custom_call_target="tpu_custom_call" | custom-call | tf_op jit(solution)/shard_map/drain/pallas_call | solution.py:448

commit v4 on v3

--- a/solution.py
+++ b/solution.py
@@ -296,9 +296,16 @@
     def over_steps(body):
         lax.fori_loop(0, steps, lambda s, carry: (body(s), carry)[1], 0)
 
+    barrier = pltpu.get_barrier_semaphore()
+    partners = [(along_fsdp(d), t) for d in partner_steps(fsdp_count)]
+    partners += [(f, along_tp(d)) for d in range(1, tp_count)]
+    for peer in partners:
+        pl.semaphore_signal(barrier, inc=1, device_id=peer, device_id_type=MESH)
+    for x in range(3):
+        stage_own(0, x).start()
+    pl.semaphore_wait(barrier, len(partners))
     for x in range(3):
         tp_start(0, x, True)
-        stage_own(0, x).start()
     over_steps(lambda s: grad_copy(s).start())
     fill_send_idx()
 
@@ -438,7 +445,7 @@
             dma((4,)),
         ],
         compiler_params=pltpu.CompilerParams(
-            has_side_effects=True, vmem_limit_bytes=22 << 20
+            has_side_effects=True, collective_id=0, vmem_limit_bytes=22 << 20
         ),
         name="restore",
     )(step, row_target.reshape(-1, LANES), saved_master, saved_first, saved_second, grad)

time: 718 us -> 714 us (level)
  no operation moved by 1% of the time
where the time goes in v4:
time: 714 us; the launch traced here: 713 us
  Pallas kernels  712 us (100%)
    pallas_call x1, Pallas kernels, per_device(): pl.pallas_call(kernel, out_shape=[pltpu.VMEM((4, steps, block_rows, LANES...  698 us

profile of v4, /device:TPU:1, one launch (start us, length us, event | category | flops | bytes accessed | tf_op | source)
XLA Modules:
  0.0 713.4 jit_solution(15998590481991237290)
XLA Ops:
  1.3 698.0 %restore.1 = (f32[4,20,1024,128]{3,2,1,0:T(8,128)S(1)}, f32[20,3,2,512,128]{4,3,2,1,0:T(8,128)}) custom-call(s32[1]{0:T(128)S(6)} %copy.10.refs_0_, s32[128,128]{1,0:T(8,128)} %bitcast.1, f32[512,5120]{1,0:T(8,128)} %refs_2_.1, f32[512,5120]{1,0:T(8,128)} %refs_3_.1, f32[512,5120]{1,0:T(8,128)} %refs_4_.1, bf16[1024,2560]{1,0:T(8,128)(2,1)} %refs_5_.1), custom_call_target="tpu_custom_call" | custom-call | tf_op jit(solution)/shard_map/restore/pallas_call | solution.py:411
  699.3 14.1 %drain.1 = (f32[1024,2560]{1,0:T(8,128)}, f32[1024,2560]{1,0:T(8,128)}, f32[1024,2560]{1,0:T(8,128)}, f32[1024,2560]{1,0:T(8,128)}) custom-call(f32[4,20,1024,128]{3,2,1,0:T(8,128)S(1)} %get-tuple-element.5.held), custom_call_target="tpu_custom_call" | custom-call | tf_op jit(solution)/shard_map/drain/pallas_call | solution.py:455

commit v5 on v4

--- a/solution.py
+++ b/solution.py
@@ -25,6 +25,38 @@
     if 1 << bits != count:
         return list(range(1, count))
     return [int(format(i, f"0{bits}b")[::-1], 2) for i in range(1, count)]
+
+
+def power_of(base, step_ref):
+    def one_bit(i, carry):
+        result, factor = carry
+        odd = lax.shift_right_logical(step_ref[0], i) & 1
+        return jnp.where(odd == 1, result * factor, result), factor * factor
+
+    return lax.fori_loop(0, 31, one_bit, (jnp.float32(1.0), jnp.float32(base)))[0]
+
+
+def adam_unit(clipped_of, step_ref, state, result):
+    first_fix = 1.0 - power_of(beta_one, step_ref)
+    second_fix = 1.0 - power_of(beta_two, step_ref)
+    tile = math.gcd(result.shape[1], 64)
+
+    def one_tile(k, carry):
+        rows = pl.ds(pl.multiple_of(k * tile, tile), tile)
+        clipped = clipped_of(rows)
+        master = state[0, rows, :]
+        first_new = beta_one * state[1, rows, :] + (1.0 - beta_one) * clipped
+        second_new = beta_two * state[2, rows, :] + (1.0 - beta_two) * clipped * clipped
+        first_hat = first_new / first_fix
+        second_hat = second_new / second_fix
+        direction = first_hat / (jnp.sqrt(second_hat) + epsilon) + weight_decay * master
+        result[0, rows, :] = master - learn_rate * direction
+        result[1, rows, :] = first_new
+        result[2, rows, :] = second_new
+        result[3, rows, :] = direction
+        return carry
+
+    lax.fori_loop(0, result.shape[1] // tile, one_tile, 0)
 
 
 def restore_kernel(count, entries, *refs):
@@ -180,14 +212,6 @@
             place_table[pl.ds(c, 1), :] = inside(jnp.transpose(column * pair + across(rank))[:1])
         to_scalars(place_table, place_idx)
 
-    def power_of(base):
-        def one_bit(i, carry):
-            result, factor = carry
-            odd = lax.shift_right_logical(step_ref[0], i) & 1
-            return jnp.where(odd == 1, result * factor, result), factor * factor
-
-        return lax.fori_loop(0, 31, one_bit, (jnp.float32(1.0), jnp.float32(base)))[0]
-
     run = math.gcd(pair, UNROLL)
 
     def gather(s, x):
@@ -226,22 +250,18 @@
 
     def adam(s):
         scale = scale_ref[...]
-        first_fix = 1.0 - power_of(beta_one)
-        second_fix = 1.0 - power_of(beta_two)
+
+        def clipped_of(rows):
+            return scale * grad[s, rows, :].astype(jnp.float32)
+
+        adam_unit(clipped_of, step_ref, out.at[:, s], out.at[:, s])
+
+    def keep_clipped():
+        scale = scale_ref[...]
 
         def one_tile(k, carry):
             rows = pl.ds(pl.multiple_of(k * tile, tile), tile)
-            clipped = scale * grad[s, rows, :].astype(jnp.float32)
-            master = out[0, s, rows, :]
-            first_new = beta_one * out[1, s, rows, :] + (1.0 - beta_one) * clipped
-            second_new = beta_two * out[2, s, rows, :] + (1.0 - beta_two) * clipped * clipped
-            first_hat = first_new / first_fix
-            second_hat = second_new / second_fix
-            direction = first_hat / (jnp.sqrt(second_hat) + epsilon) + weight_decay * master
-            out[0, s, rows, :] = master - learn_rate * direction
-            out[1, s, rows, :] = first_new
-            out[2, s, rows, :] = second_new
-            out[3, s, rows, :] = direction
+            out[3, steps - 1, rows, :] = scale * grad[steps - 1, rows, :].astype(jnp.float32)
             return carry
 
         lax.fori_loop(0, block_rows // tile, one_tile, 0)
@@ -330,6 +350,7 @@
         total = jnp.sum(summed(from_fsdp, fsdp_count), axis=1, keepdims=True)
         scale = jnp.minimum(1.0, math.sqrt(entries) / jnp.sqrt(total))
         scale_ref[...] = jnp.broadcast_to(scale, scale_ref.shape)
+        keep_clipped()
 
     def step(s, carry):
         for x in range(3):
@@ -362,7 +383,7 @@
         @pl.when(s >= 1)
         def _():
             pl.when(s == 1)(end_total)
-            adam(s - 1)
+            pl.when(s < steps)(lambda: adam(s - 1))
 
         return carry
 
@@ -375,19 +396,23 @@
     partial_wait(1, 0)
 
 
-def drain_kernel(held, *refs):
-    outs, sem = refs[:-1], refs[-1]
-    copies = [
-        pltpu.make_async_copy(
-            held.at[i, u], out.at[:, u * LANES : (u + 1) * LANES], sem.at[i, u]
-        )
-        for i, out in enumerate(outs)
-        for u in range(held.shape[1])
-    ]
-    for copy in copies:
-        copy.start()
-    for copy in copies:
-        copy.wait()
+def drain_kernel(step_ref, held, *refs):
+    outs, (last, sem) = refs[:4], refs[4:]
+    final = held.shape[1] - 1
+
+    def copy(i, u):
+        source = last.at[i] if u == final else held.at[i, u]
+        return pltpu.make_async_copy(source, outs[i].at[:, u * LANES : (u + 1) * LANES], sem.at[i, u])
+
+    earlier = [copy(i, u) for i in range(4) for u in range(final)]
+    for one in earlier:
+        one.start()
+    adam_unit(lambda rows: held[3, final, rows, :], step_ref, held.at[:, final], last)
+    latest = [copy(i, final) for i in range(4)]
+    for one in latest:
+        one.start()
+    for one in earlier + latest:
+        one.wait()
 
 
 def per_device(entries, saved_master, saved_first, saved_second, grad, row_target, step):
@@ -455,12 +480,15 @@
         pl.pallas_call(
             drain_kernel,
             out_shape=[out] * 4,
-            in_specs=[pl.BlockSpec(memory_space=pl.ANY)],
+            in_specs=[smem, vmem],
             out_specs=[hbm] * 4,
-            scratch_shapes=[dma((4, steps))],
-            compiler_params=pltpu.CompilerParams(vmem_limit_bytes=1 << 20),
+            scratch_shapes=[
+                pltpu.VMEM((4, block_rows, LANES), wide),
+                dma((4, steps)),
+            ],
+            compiler_params=pltpu.CompilerParams(vmem_limit_bytes=4 << 20),
             name="drain",
-        )(held)
+        )(step, held)
     )
 
 

time: 714 us -> 712 us (level)
  no operation moved by 1% of the time
where the time goes in v5:
time: 712 us
  Pallas kernels  711 us (100%)
    pallas_call x1, Pallas kernels, per_device(): pl.pallas_call(kernel, out_shape=[pltpu.VMEM((4, steps, block_rows, LANES...  697 us

profile of v5, /device:TPU:1, one launch (start us, length us, event | category | flops | bytes accessed | tf_op | source)
XLA Modules:
  0.0 712.2 jit_solution(11989615401997477372)
XLA Ops:
  1.3 696.8 %restore.1 = (f32[4,20,1024,128]{3,2,1,0:T(8,128)S(1)}, f32[20,3,2,512,128]{4,3,2,1,0:T(8,128)}) custom-call(s32[1]{0:T(128)S(6)} %copy.10.refs_0_.step_ref, s32[128,128]{1,0:T(8,128)} %bitcast.1, f32[512,5120]{1,0:T(8,128)} %refs_2_.1, f32[512,5120]{1,0:T(8,128)} %refs_3_.1, f32[512,5120]{1,0:T(8,128)} %refs_4_.1, bf16[1024,2560]{1,0:T(8,128)(2,1)} %refs_5_.1), custom_call_target="tpu_custom_call" | custom-call | tf_op jit(solution)/shard_map/restore/pallas_call | solution.py:436
  698.1 14.1 %drain.1 = (f32[1024,2560]{1,0:T(8,128)}, f32[1024,2560]{1,0:T(8,128)}, f32[1024,2560]{1,0:T(8,128)}, f32[1024,2560]{1,0:T(8,128)}) custom-call(s32[1]{0:T(128)S(6)} %copy.10.refs_0_.step_ref, f32[4,20,1024,128]{3,2,1,0:T(8,128)S(1)} %get-tuple-element.5.held), custom_call_target="tpu_custom_call" | custom-call | tf_op jit(solution)/shard_map/drain/pallas_call | solution.py:480
